TPU v7x, 512 devices: a whole 4x8x8 slice. The times are simulated.
512 devices in a mesh: mem: 32 (over y, z_lo, core), row: 4 (over x), col: 4 (over z_hi).
Axes of the slice: x: 4, y: 8, z: 8 (z_hi: 4, z_lo: 2; z = z_hi * 2 + z_lo), core: 2. Of those that a mesh axis runs over, the one named last changes fastest.
Arguments:
- background_sample: float32 [64, 4, 32, 32, 512], P('mem', None, None, 'row', 'col'), may hold values from -6 to 6
- coupling: float32 [4, 4], replicated, may hold values from -0.6 to 0.6
- diffusion: float32 [32], replicated, may hold values from 0.02 to 0.12
- wind_row: float32 [32], replicated, may hold values from -0.4 to 0.4
- wind_col: float32 [32], replicated, may hold values from -0.4 to 0.4
- observed_entry_index: int32 [64, 32, 512], P(None, 'row', ('col', 'mem')), may hold values from 0 to 127
- obs_value: float32 [64, 32, 512], P(None, 'row', ('col', 'mem')), may hold values from -6 to 6
- obs_weight: float32 [64, 32, 512], P(None, 'row', ('col', 'mem')), may hold values from 0.25 to 4
Outputs:
- analysis: float32 [64, 4, 32, 32, 512], P(None, None, None, 'row', ('col', 'mem'))
Inputs may be any that keep to these rules, and one draw needn't show every extreme that they name: observed_entry_index names an entry of a column as variable times 32 plus level.
All inputs are finite; a program needn't handle non-finite values.
Results may differ from a plain program's by a relative error of at most 0.0003.
Values sent between devices are 32-bit elements; how exact they have to be, the bound alone decides.
No kernel may reach another device: no remote copies, remote signals or barrier semaphores. Data moves between devices by JAX's collectives and lax.ppermute only.
A program may use at most 64 MiB of HBM per device.

v0:
```python
import jax
import jax.numpy as jnp
from jax import lax
from jax.experimental import pallas as pl
from jax.experimental.pallas import tpu as pltpu
from jax.sharding import PartitionSpec as P

HALO = 4
EDGE = 16
DEPTH = (14, 12, 10, 8)
GROUP = 4
GRANT = pltpu.CompilerParams(vmem_limit_bytes=14 * 2**20)
NEWTON = (2.25, -2.4375, 1.6875, -0.5625, 0.0625)


def turn_kernel(block, top, bottom, west, east):
    members, entries, rows, cols = block.shape
    flat = block.reshape(members, entries * rows, cols)
    for m in range(members):
        for i in range(rows):
            plane = flat[m, pl.ds(i, entries, stride=rows), :].T
            half = top if i < HALO else bottom
            half[m, i % HALO] = plane
            west[m, i] = plane[:HALO]
            east[m, i] = plane[cols - HALO :]


def turn(block):
    members, variables, levels, rows, cols = block.shape
    entries = variables * levels
    half = jax.ShapeDtypeStruct((members, HALO, cols, entries), jnp.float32)
    side = jax.ShapeDtypeStruct((members, rows, HALO, entries), jnp.float32)
    return pl.pallas_call(
        turn_kernel,
        out_shape=[half, half, side, side],
        compiler_params=GRANT,
        name="turn",
    )(block.reshape(members, entries, rows, cols))


def forecast_kernel(
    coupling, rates, top, bottom, north, south, west, east, corner_n, corner_s, out, state, slope, mixer
):
    members, _, cols, entries = top.shape
    dests, listed, _ = out.shape
    cells = listed // members
    variables = coupling.shape[0]
    levels = entries // variables
    share = cols // dests
    rows = 2 * HALO
    last = EDGE + cols
    inside = [
        jnp.where(test, 1.0, 0.0)
        for test in (
            lax.axis_index("row") > 0,
            lax.axis_index("row") < lax.axis_size("row") - 1,
            lax.axis_index("col") > 0,
            lax.axis_index("col") < lax.axis_size("col") - 1,
        )
    ]
    diffusion, wind_row, wind_col = (
        jnp.concatenate([rates[k : k + 1]] * variables, axis=1) for k in range(3)
    )
    c_n, c_s = (diffusion + 0.5 * wind_row, diffusion - 0.5 * wind_row)
    c_w, c_e = (diffusion + 0.5 * wind_col, diffusion - 0.5 * wind_col)
    source = lax.broadcasted_iota(jnp.int32, (entries, entries), 0)
    target = lax.broadcasted_iota(jnp.int32, (entries, entries), 1)
    mixing = jnp.where(source == target, -4.0 * diffusion, 0.0)
    for v in range(variables):
        for w in range(variables):
            hit = (target - source == levels * (v - w)) & (target // levels == v)
            mixing += jnp.where(hit, coupling[v, w], 0.0)
    mixer[...] = jnp.concatenate([jnp.concatenate(halves(mixing), axis=1)] * 2, axis=0)

    def tendency(field, i, deep, start, size):
        here = field[pl.ds(i, deep), pl.ds(start, size), :]
        parts = jnp.concatenate(halves(here), axis=2).reshape(deep * size, 2 * entries)
        both = lax.dot_general(
            parts, mixer[...], (((1,), (0,)), ((), ())), preferred_element_type=jnp.float32
        )
        total = c_n * field[pl.ds(i - 1, deep), pl.ds(start, size), :]
        total += c_s * field[pl.ds(i + 1, deep), pl.ds(start, size), :]
        total += c_w * field[pl.ds(i, deep), pl.ds(start - 1, size), :]
        total += c_e * field[pl.ds(i, deep), pl.ds(start + 1, size), :]
        both = both.reshape(deep, size, 2 * entries)
        return here, total + (both[:, :, :entries] + both[:, :, entries:])

    def masked(value, i):
        deep, size, _ = value.shape
        row = i + lax.broadcasted_iota(jnp.int32, (deep, 1, 1), 0)
        value = value * jnp.where(row < HALO, inside[0], jnp.where(row >= 3 * HALO, inside[1], 1.0))
        where = first + lax.broadcasted_iota(jnp.int32, (1, size, 1), 1)
        return value * jnp.where(where < EDGE, inside[2], jnp.where(where >= last, inside[3], 1.0))

    first, wide = (EDGE - 8, cols + 16)

    def rates_of(low, high, deep):
        def step(b, carry):
            i = low + deep * b
            here, total = tendency(state, i, deep, first, wide)
            slope[pl.ds(i, deep), pl.ds(first, wide), :] = masked(total, i)
            return carry

        lax.fori_loop(0, (high - low) // deep, step, 0)

    def update(low, high, deep):
        def step(b, carry):
            i = low + deep * b
            here, total = tendency(slope, i, deep, first, wide)
            new = state[pl.ds(i, deep), pl.ds(first, wide), :] + here + 0.5 * total
            state[pl.ds(i, deep), pl.ds(first, wide), :] = masked(new, i)
            return carry

        lax.fori_loop(0, (high - low) // deep, step, 0)

    def member(m, carry):
        for i in range(HALO):
            state[i, EDGE:last] = north[m, i]
            state[HALO + i, EDGE:last] = top[m, i]
            state[2 * HALO + i, EDGE:last] = bottom[m, i]
            state[3 * HALO + i, EDGE:last] = south[m, i]
            state[i, EDGE - HALO : EDGE] = corner_n[m, i, :HALO]
            state[i, last : last + HALO] = corner_n[m, i, HALO:]
            state[3 * HALO + i, EDGE - HALO : EDGE] = corner_s[m, i, :HALO]
            state[3 * HALO + i, last : last + HALO] = corner_s[m, i, HALO:]
        for i in range(rows):
            state[HALO + i, EDGE - HALO : EDGE] = west[m, i]
            state[HALO + i, last : last + HALO] = east[m, i]
        rates_of(1, 15, DEPTH[0])
        update(2, 14, DEPTH[1])
        rates_of(3, 13, DEPTH[2])
        for i in range(0, rows, DEPTH[3]):
            here, total = tendency(slope, HALO + i, DEPTH[3], EDGE, cols)
            new = state[HALO + i : HALO + i + DEPTH[3], EDGE:last] + here + 0.5 * total
            for r in range(DEPTH[3]):
                for d in range(dests):
                    out[d, pl.ds(m * cells + (i + r) * share, share), :] = new[r, d * share : (d + 1) * share]
        return carry

    lax.fori_loop(0, members, member, 0)


def forecast(coupling, rates, top, bottom, north, south, west, east, corner_n, corner_s, dests):
    members, _, cols, entries = top.shape
    cells = 2 * HALO * cols // dests
    return pl.pallas_call(
        forecast_kernel,
        in_specs=[pl.BlockSpec(memory_space=pltpu.SMEM)] + [pl.BlockSpec()] * 9,
        out_shape=jax.ShapeDtypeStruct((dests, members * cells, entries), jnp.float32),
        scratch_shapes=[pltpu.VMEM((4 * HALO, cols + 2 * EDGE, entries), jnp.float32)] * 2
        + [pltpu.VMEM((2 * entries, 2 * entries), jnp.bfloat16)],
        compiler_params=GRANT,
        name="forecast",
    )(coupling, rates, top, bottom, north, south, west, east, corner_n, corner_s)


def weigh_kernel(index, value, weight, total, pulled):
    cells, observations = index.shape
    entries = total.shape[1]
    entry = lax.broadcasted_iota(jnp.int32, (cells, entries), 1)
    w = weight[...]
    wv = w * value[...]
    acc = jnp.zeros((cells, entries), jnp.float32)
    acc_v = jnp.zeros((cells, entries), jnp.float32)
    named = index[...]
    for k in range(observations):
        hit = jnp.broadcast_to(named[:, k : k + 1], (cells, entries)) == entry
        acc += jnp.where(hit, jnp.broadcast_to(w[:, k : k + 1], (cells, entries)), 0.0)
        acc_v += jnp.where(hit, jnp.broadcast_to(wv[:, k : k + 1], (cells, entries)), 0.0)
    total[...] = acc
    pulled[...] = acc_v


def weigh(index, value, weight, entries):
    shape = jax.ShapeDtypeStruct((index.shape[0], entries), jnp.float32)
    return pl.pallas_call(weigh_kernel, out_shape=[shape, shape], compiler_params=GRANT, name="weigh")(
        index, value, weight
    )


def halves(value):
    high = value.astype(jnp.bfloat16)
    return high, (value - high.astype(jnp.float32)).astype(jnp.bfloat16)


def product(a, b, turned=False):
    (ah, al), (bh, bl) = (a, b)
    dot = lambda u, v: lax.dot_general(
        u, v, (((1,), (1 if turned else 0,)), ((), ())), preferred_element_type=jnp.float32
    )
    both = dot(jnp.concatenate([ah, ah], axis=1), jnp.concatenate([bh, bl], axis=1 if turned else 0))
    return both + dot(al, bh)


def analyse_kernel(block, total, pulled, out):
    cells = total.shape[0]
    members = block.shape[0] // cells
    entries = block.shape[1]
    pair = 2 * members
    row_id = lax.broadcasted_iota(jnp.int32, (pair, pair), 0)
    col_id = lax.broadcasted_iota(jnp.int32, (pair, pair), 1)
    eye = (row_id == col_id).astype(jnp.float32)
    same = ((row_id < members) == (col_id < members)).astype(jnp.float32)
    left = lax.broadcasted_iota(jnp.int32, (1, pair), 1) < members
    n0, n1, n2, n3, n4 = NEWTON
    spread = lambda row: jnp.broadcast_to(row, (members, entries))

    def first(cell):
        x = [block[pl.ds(cell + u, members, stride=cells), :] for u in range(2)]
        mean = [jnp.sum(v, axis=0, keepdims=True) * (1.0 / members) for v in x]
        weight = [total[pl.ds(cell + u, 1), :] for u in range(2)]
        pull = [pulled[pl.ds(cell + u, 1), :] - mean[u] * weight[u] for u in range(2)]
        pert = [x[u] - mean[u] for u in range(2)]
        scaled = jnp.concatenate([pert[u] * weight[u] for u in range(2)], axis=0)
        gain = jnp.concatenate(
            [jnp.sum(pert[u] * pull[u], axis=1, keepdims=True) for u in range(2)], axis=0
        )
        system = product(halves(scaled), halves(jnp.concatenate(pert, axis=0)), turned=True)
        return jnp.concatenate(x, axis=0).T, gain, system * same + (members - 1.0) * eye

    def second(state):
        x_turned, gain, system = state
        square = jnp.sum(system * system, axis=0, keepdims=True)
        halved = [
            jnp.sum(jnp.where(side, square, 0.0), axis=1, keepdims=True) for side in (left, ~left)
        ]
        scale_inv = lax.rsqrt(jnp.where(left, halved[0], halved[1]))
        a = system * scale_inv
        parts = halves(a)
        return x_turned, gain, scale_inv, a, product(parts, parts)

    def third(state):
        x_turned, gain, scale_inv, a, b = state
        inverse = n0 * eye + n1 * a + n2 * b + product(halves(b), halves(n3 * a + n4 * b))
        return x_turned, gain, scale_inv, inverse

    def fourth(state):
        x_turned, gain, scale_inv, inverse = state
        half_vec = jnp.sum(inverse * gain, axis=0, keepdims=True)
        centre = jnp.sum(inverse * half_vec, axis=1, keepdims=True)
        weights = inverse * jnp.sqrt((members - 1.0) * scale_inv) + centre * (same * scale_inv)
        rest = (1.0 - jnp.sum(weights, axis=0, keepdims=True)) * (1.0 / members)
        return product(halves(x_turned), halves(weights + rest * same))

    def step(g, carry):
        cell = [g * (2 * GROUP) + 2 * u for u in range(GROUP)]
        states = [first(c) for c in cell]
        states = [second(s) for s in states]
        states = [third(s) for s in states]
        results = [fourth(s) for s in states]
        for c, result in zip(cell, results):
            out[pl.ds(c, entries, stride=cells), :] = result[:, :members]
            out[pl.ds(c + 1, entries, stride=cells), :] = result[:, members:]
        return carry

    lax.fori_loop(0, cells // (2 * GROUP), step, 0)


def analyse(block, total, pulled):
    cells, entries = total.shape
    members = block.shape[0] // cells
    return pl.pallas_call(
        analyse_kernel,
        out_shape=jax.ShapeDtypeStruct((entries * cells, members), jnp.float32),
        compiler_params=GRANT,
        name="analyse",
    )(block, total, pulled)


def neighbours(axis):
    up = [(i, i + 1) for i in range(lax.axis_size(axis) - 1)]
    return up, [(j, i) for i, j in up]


def body(
    background_sample,
    coupling,
    diffusion,
    wind_row,
    wind_col,
    observed_entry_index,
    obs_value,
    obs_weight,
):
    members_here, variables, levels, rows, cols = background_sample.shape
    entries = variables * levels
    dests = lax.axis_size("mem")
    top, bottom, own_w, own_e = turn(background_sample)
    col_up, col_down = neighbours("col")
    row_up, row_down = neighbours("row")
    west = lax.ppermute(own_e, "col", col_up)
    east = lax.ppermute(own_w, "col", col_down)
    north = lax.ppermute(bottom, "row", row_up)
    south = lax.ppermute(top, "row", row_down)
    sides = jnp.concatenate([west, east], axis=2)
    corner_n = lax.ppermute(sides[:, HALO:], "row", row_up)
    corner_s = lax.ppermute(sides[:, :HALO], "row", row_down)

    rates = jnp.stack([diffusion, wind_row, wind_col])
    sent = forecast(
        coupling, rates, top, bottom, north, south, west, east, corner_n, corner_s, dests
    )
    moved = lax.all_to_all(sent, "mem", split_axis=0, concat_axis=0, tiled=True)
    cells = rows * cols // dests
    members = dests * members_here

    def listed(x):
        return jnp.transpose(x, (1, 2, 0)).reshape(cells, x.shape[0])

    total, pulled = weigh(
        listed(observed_entry_index), listed(obs_value), listed(obs_weight), entries
    )
    result = analyse(moved.reshape(members * cells, entries), total, pulled)
    result = result.reshape(variables, levels, rows, cols // dests, members)
    return jnp.transpose(result, (4, 0, 1, 2, 3))


def solution(mesh):
    obs = P(None, "row", ("col", "mem"))
    return jax.shard_map(
        body,
        mesh=mesh,
        in_specs=(P("mem", None, None, "row", "col"), P(), P(), P(), P(), obs, obs, obs),
        out_specs=P(None, None, None, "row", ("col", "mem")),
        check_vma=False,
    )
```

profile of v0, /device:TPU:1, one launch (start us, length us, event | category | flops | bytes accessed | tf_op | source)
XLA Modules:
  0.0 83.0 jit_solution(1437376804005271665)
XLA Ops:
  0.0 0.0 copy-start
  0.0 1.2 %copy-done = f32[2,4,32,8,128]{4,3,2,1,0:T(8,128)S(1)} copy-done((f32[2,4,32,8,128]{4,3,2,1,0:T(8,128)S(1)}, f32[2,4,32,8,128]{4,3,2,1,0:T(8,128)}, u32[]{:S(2)}) %copy-start) | copy-done | bytes 1048600
  1.2 0.3 turn.1
  1.6 4.0 %collective-permute-start = (f32[2,4,128,128]{3,2,1,0:T(8,128)S(1)}, f32[2,4,128,128]{3,2,1,0:T(8,128)S(1)}, u32[]{:S(2)}, u32[]{:S(2)}) collective-permute-start(f32[2,4,128,128]{3,2,1,0:T(8,128)S(1)} %get-tuple-element.12.bottom), channel_id=1, source_target_pairs={{0,4},{4,8},{8,12},{1,5},{5,9},{9,13},{2,6},{6,10},{10,14},{3,7},{... | collective-permute-start | bytes 1572872 | tf_op jit(solution)/shard_map/ppermute | solution.py:293
  5.5 1.3 %collective-permute-start.1 = (f32[2,4,128,128]{3,2,1,0:T(8,128)S(1)}, f32[2,4,128,128]{3,2,1,0:T(8,128)S(1)}, u32[]{:S(2)}, u32[]{:S(2)}) collective-permute-start(f32[2,4,128,128]{3,2,1,0:T(8,128)S(1)} %get-tuple-element.11.top), channel_id=1, source_target_pairs={{4,0},{8,4},{12,8},{5,1},{9,5},{13,9},{6,2},{10,6},{14,10},{7,3},{... | collective-permute-start | bytes 1572872 | tf_op jit(solution)/shard_map/ppermute | solution.py:294
  6.8 5.8 %collective-permute-start.2 = (f32[2,8,4,128]{3,2,1,0:T(4,128)S(1)}, f32[2,8,4,128]{3,2,1,0:T(4,128)S(1)}, u32[]{:S(2)}, u32[]{:S(2)}) collective-permute-start(f32[2,8,4,128]{3,2,1,0:T(4,128)S(1)} %get-tuple-element.13), channel_id=1, source_target_pairs={{0,1},{1,2},{2,3},{4,5},{5,6},{6,7},{8,9},{9,10},{10,11},{12,13},{... | collective-permute-start | bytes 98312 | tf_op jit(solution)/shard_map/ppermute | solution.py:291
  12.6 1.3 %collective-permute-start.3 = (f32[2,8,4,128]{3,2,1,0:T(4,128)S(1)}, f32[2,8,4,128]{3,2,1,0:T(4,128)S(1)}, u32[]{:S(2)}, u32[]{:S(2)}) collective-permute-start(f32[2,8,4,128]{3,2,1,0:T(4,128)S(1)} %get-tuple-element.14), channel_id=1, source_target_pairs={{1,0},{2,1},{3,2},{5,4},{6,5},{7,6},{9,8},{10,9},{11,10},{13,12},{... | collective-permute-start | bytes 98312 | tf_op jit(solution)/shard_map/ppermute | solution.py:292
  13.9 0.0 collective-permute-done.2.west
  14.0 7.0 %collective-permute-done.3.east = f32[2,8,4,128]{3,2,1,0:T(4,128)S(1)} collective-permute-done((f32[2,8,4,128]{3,2,1,0:T(4,128)S(1)}, f32[2,8,4,128]{3,2,1,0:T(4,128)S(1)}, u32[]{:S(2)}, u32[]{:S(2)}) %collective-permute-start.3) | collective-permute-done | bytes 32800 | tf_op jit(solution)/shard_map/ppermute | solution.py:292
  21.0 4.0 %collective-permute-start.4 = (f32[2,4,8,128]{3,2,1,0:T(8,128)S(1)}, f32[2,4,8,128]{3,2,1,0:T(8,128)S(1)}, u32[]{:S(2)}, u32[]{:S(2)}) collective-permute-start(f32[2,4,8,128]{3,2,1,0:T(8,128)S(1)} %get-tuple-element.18), channel_id=1, source_target_pairs={{0,4},{4,8},{8,12},{1,5},{5,9},{9,13},{2,6},{6,10},{10,14},{3,7},{... | collective-permute-start | bytes 98312 | tf_op jit(solution)/shard_map/ppermute | solution.py:296
  25.0 1.3 %collective-permute-start.5 = (f32[2,4,8,128]{3,2,1,0:T(8,128)S(1)}, f32[2,4,8,128]{3,2,1,0:T(8,128)S(1)}, u32[]{:S(2)}, u32[]{:S(2)}) collective-permute-start(f32[2,4,8,128]{3,2,1,0:T(8,128)S(1)} %get-tuple-element.17), channel_id=1, source_target_pairs={{4,0},{8,4},{12,8},{5,1},{9,5},{13,9},{6,2},{10,6},{14,10},{7,3},{... | collective-permute-start | bytes 98312 | tf_op jit(solution)/shard_map/ppermute | solution.py:297
  26.3 0.7 pad_maximum_fusion.1.rates
  27.0 0.0 copy-start.1
  27.0 0.0 copy-start.2
  27.0 0.0 copy-start.3
  27.0 0.0 collective-permute-done.4.corner_n
  27.0 2.6 %collective-permute-done.5.corner_s = f32[2,4,8,128]{3,2,1,0:T(8,128)S(1)} collective-permute-done((f32[2,4,8,128]{3,2,1,0:T(8,128)S(1)}, f32[2,4,8,128]{3,2,1,0:T(8,128)S(1)}, u32[]{:S(2)}, u32[]{:S(2)}) %collective-permute-start.5) | collective-permute-done | bytes 32800 | tf_op jit(solution)/shard_map/ppermute | solution.py:297
  29.6 0.0 collective-permute-done.north
  29.6 0.0 collective-permute-done.1.south
  29.6 0.0 copy-start.4
  29.7 0.7 copy-done.4
  30.3 4.9 %forecast.1 = f32[32,64,128]{2,1,0:T(8,128)} custom-call(f32[4,4]{1,0:T(4,128)S(1)} %copy-done.4, f32[3,32]{1,0:T(4,128)S(1)} %pad_maximum_fusion.1.rates, f32[2,4,128,128]{3,2,1,0:T(8,128)S(1)} %get-tuple-element.11.top, f32[2,4,128,128]{3,2,1,0:T(8,128)S(1)} %get-tuple-element.12.bottom, f32[2,4,128,128]{3,2,1,0:T(8,128)S(1)} %collective-permute-done.north, ...), custom_call_target="tpu_custom_call" | custom-call | tf_op jit(solution)/shard_map/forecast/pallas_call | solution.py:146
  35.3 12.0 %all-to-all-start = ((f32[32,64,128]{2,1,0:T(8,128)}), f32[32,64,128]{2,1,0:T(8,128)S(1)}, u32[]{:S(2)}, u32[]{:S(2)}) async-start(f32[32,64,128]{2,1,0:T(8,128)} %forecast.1), calls=%async_computation | async-start | bytes 2097152 | tf_op jit(solution)/shard_map/all_to_all | solution.py:303
  47.3 0.0 copy-done.1
  47.3 0.0 copy-done.2
  47.3 0.0 copy-done.3
  47.3 1.0 %weigh.1 = (f32[32,128]{1,0:T(8,128)S(1)}, f32[32,128]{1,0:T(8,128)S(1)}) custom-call(s32[32,64]{1,0:T(8,128)S(1)} %bitcast.19, f32[32,64]{1,0:T(8,128)S(1)} %bitcast.20, f32[32,64]{1,0:T(8,128)S(1)} %bitcast.21), custom_call_target="tpu_custom_call" | custom-call | tf_op jit(solution)/shard_map/weigh/pallas_call | solution.py:176
  48.3 27.1 %all-to-all-done = f32[32,64,128]{2,1,0:T(8,128)S(1)} async-done(((f32[32,64,128]{2,1,0:T(8,128)}), f32[32,64,128]{2,1,0:T(8,128)S(1)}, u32[]{:S(2)}, u32[]{:S(2)}) %all-to-all-start) | async-done | bytes 1048608 | tf_op jit(solution)/shard_map/all_to_all | solution.py:303
  75.3 7.7 %analyse.1 = f32[4096,64]{1,0:T(8,128)} custom-call(f32[2048,128]{1,0:T(8,128)S(1)} %bitcast.17, f32[32,128]{1,0:T(8,128)S(1)} %get-tuple-element.15.total, f32[32,128]{1,0:T(8,128)S(1)} %get-tuple-element.16.pulled), custom_call_target="tpu_custom_call" | custom-call | tf_op jit(solution)/shard_map/analyse/pallas_call | solution.py:262
  (1 shorter events, 0.0 us)
Async XLA Ops:
  0.0 1.2 %copy-start = (f32[2,4,32,8,128]{4,3,2,1,0:T(8,128)S(1)}, f32[2,4,32,8,128]{4,3,2,1,0:T(8,128)}, u32[]{:S(2)}) copy-start(f32[2,4,32,8,128]{4,3,2,1,0:T(8,128)} %param.8) | copy-start | bytes 3145732
  1.6 28.1 %collective-permute-start = (f32[2,4,128,128]{3,2,1,0:T(8,128)S(1)}, f32[2,4,128,128]{3,2,1,0:T(8,128)S(1)}, u32[]{:S(2)}, u32[]{:S(2)}) collective-permute-start(f32[2,4,128,128]{3,2,1,0:T(8,128)S(1)} %get-tuple-element.12.bottom), channel_id=1, source_target_pairs={{0,4},{4,8},{8,12},{1,5},{5,9},{9,13},{2,6},{6,10},{10,14},{3,7},{... | collective-permute-start | bytes 1572872 | tf_op jit(solution)/shard_map/ppermute | solution.py:293
  5.5 24.1 %collective-permute-start.1 = (f32[2,4,128,128]{3,2,1,0:T(8,128)S(1)}, f32[2,4,128,128]{3,2,1,0:T(8,128)S(1)}, u32[]{:S(2)}, u32[]{:S(2)}) collective-permute-start(f32[2,4,128,128]{3,2,1,0:T(8,128)S(1)} %get-tuple-element.11.top), channel_id=1, source_target_pairs={{4,0},{8,4},{12,8},{5,1},{9,5},{13,9},{6,2},{10,6},{14,10},{7,3},{... | collective-permute-start | bytes 1572872 | tf_op jit(solution)/shard_map/ppermute | solution.py:294
  6.8 7.1 %collective-permute-start.2 = (f32[2,8,4,128]{3,2,1,0:T(4,128)S(1)}, f32[2,8,4,128]{3,2,1,0:T(4,128)S(1)}, u32[]{:S(2)}, u32[]{:S(2)}) collective-permute-start(f32[2,8,4,128]{3,2,1,0:T(4,128)S(1)} %get-tuple-element.13), channel_id=1, source_target_pairs={{0,1},{1,2},{2,3},{4,5},{5,6},{6,7},{8,9},{9,10},{10,11},{12,13},{... | collective-permute-start | bytes 98312 | tf_op jit(solution)/shard_map/ppermute | solution.py:291
  12.6 8.3 %collective-permute-start.3 = (f32[2,8,4,128]{3,2,1,0:T(4,128)S(1)}, f32[2,8,4,128]{3,2,1,0:T(4,128)S(1)}, u32[]{:S(2)}, u32[]{:S(2)}) collective-permute-start(f32[2,8,4,128]{3,2,1,0:T(4,128)S(1)} %get-tuple-element.14), channel_id=1, source_target_pairs={{1,0},{2,1},{3,2},{5,4},{6,5},{7,6},{9,8},{10,9},{11,10},{13,12},{... | collective-permute-start | bytes 98312 | tf_op jit(solution)/shard_map/ppermute | solution.py:292
  21.0 6.0 %collective-permute-start.4 = (f32[2,4,8,128]{3,2,1,0:T(8,128)S(1)}, f32[2,4,8,128]{3,2,1,0:T(8,128)S(1)}, u32[]{:S(2)}, u32[]{:S(2)}) collective-permute-start(f32[2,4,8,128]{3,2,1,0:T(8,128)S(1)} %get-tuple-element.18), channel_id=1, source_target_pairs={{0,4},{4,8},{8,12},{1,5},{5,9},{9,13},{2,6},{6,10},{10,14},{3,7},{... | collective-permute-start | bytes 98312 | tf_op jit(solution)/shard_map/ppermute | solution.py:296
  25.0 4.7 %collective-permute-start.5 = (f32[2,4,8,128]{3,2,1,0:T(8,128)S(1)}, f32[2,4,8,128]{3,2,1,0:T(8,128)S(1)}, u32[]{:S(2)}, u32[]{:S(2)}) collective-permute-start(f32[2,4,8,128]{3,2,1,0:T(8,128)S(1)} %get-tuple-element.17), channel_id=1, source_target_pairs={{4,0},{8,4},{12,8},{5,1},{9,5},{13,9},{6,2},{10,6},{14,10},{7,3},{... | collective-permute-start | bytes 98312 | tf_op jit(solution)/shard_map/ppermute | solution.py:297
  27.0 20.3 %copy-start.1 = (s32[64,8,4]{0,2,1:T(4,128)S(1)}, s32[64,8,4]{0,2,1:T(4,128)}, u32[]{:S(2)}) copy-start(s32[64,8,4]{0,2,1:T(4,128)} %param.13) | copy-start | bytes 24580
  27.0 20.3 %copy-start.2 = (f32[64,8,4]{0,2,1:T(4,128)S(1)}, f32[64,8,4]{0,2,1:T(4,128)}, u32[]{:S(2)}) copy-start(f32[64,8,4]{0,2,1:T(4,128)} %param.14) | copy-start | bytes 24580
  27.0 20.3 %copy-start.3 = (f32[64,8,4]{0,2,1:T(4,128)S(1)}, f32[64,8,4]{0,2,1:T(4,128)}, u32[]{:S(2)}) copy-start(f32[64,8,4]{0,2,1:T(4,128)} %param.15) | copy-start | bytes 24580
  29.6 0.7 copy-start.4
  35.3 40.1 %all-to-all-start = ((f32[32,64,128]{2,1,0:T(8,128)}), f32[32,64,128]{2,1,0:T(8,128)S(1)}, u32[]{:S(2)}, u32[]{:S(2)}) async-start(f32[32,64,128]{2,1,0:T(8,128)} %forecast.1), calls=%async_computation | async-start | bytes 2097152 | tf_op jit(solution)/shard_map/all_to_all | solution.py:303
where the time goes:
time: 83.4 us; the launch traced here: 83 us
  waiting for transfers between devices  36.7 us (44%)
  starting transfers between devices  29.6 us (35%)
  Pallas kernels  13.9 us (17%)
  local copies, waits for them, and re-layouts  1.92 us (2%)
    all_to_all x1, waiting for transfers between devices, body(): moved = lax.all_to_all(sent, 'mem', split_axis=0, concat_axis=0, tiled=True)  27.1 us
    all_to_all x1, starting transfers between devices, body(): moved = lax.all_to_all(sent, 'mem', split_axis=0, concat_axis=0, tiled=True)  12 us
    pallas_call x1, Pallas kernels, analyse(): pl.pallas_call(analyse_kernel, out_shape=jax.ShapeDtypeStruct((entries *...  7.69 us
    ppermute x1, waiting for transfers between devices, body(): east = lax.ppermute(own_w, 'col', col_down)  7.01 us
    ppermute x1, starting transfers between devices, body(): west = lax.ppermute(own_e, 'col', col_up)  5.81 us
    pallas_call x1, Pallas kernels, forecast(): pl.pallas_call(forecast_kernel, in_specs=[pl.BlockSpec(memory_space=pltpu...  4.95 us
    ppermute x1, starting transfers between devices, body(): corner_n = lax.ppermute(sides[:, HALO:], 'row', row_up)  3.99 us
    ppermute x1, starting transfers between devices, body(): north = lax.ppermute(bottom, 'row', row_up)  3.97 us
  transfers between devices with their start and end apart: 7, of which 3 were waited for; matrix products, arithmetic and copies ran while one was open for 1% of the time, Pallas kernels for 1%

commit v1 on v0

--- a/solution.py
+++ b/solution.py
@@ -8,7 +8,9 @@
 HALO = 4
 EDGE = 16
 DEPTH = (14, 12, 10, 8)
-GROUP = 4
+GROUP = 8
+IN_STEP = 33
+OUT_STEP = 40
 GRANT = pltpu.CompilerParams(vmem_limit_bytes=14 * 2**20)
 NEWTON = (2.25, -2.4375, 1.6875, -0.5625, 0.0625)
 
@@ -39,13 +41,13 @@
 
 
 def forecast_kernel(
-    coupling, rates, top, bottom, north, south, west, east, corner_n, corner_s, out, state, slope, mixer
+    rates, top, bottom, north, south, west, east, corner_n, corner_s, out, state, slope, mixer
 ):
     members, _, cols, entries = top.shape
     dests, listed, _ = out.shape
     cells = listed // members
-    variables = coupling.shape[0]
-    levels = entries // variables
+    levels = rates.shape[1]
+    variables = entries // levels
     share = cols // dests
     rows = 2 * HALO
     last = EDGE + cols
@@ -69,7 +71,7 @@
     for v in range(variables):
         for w in range(variables):
             hit = (target - source == levels * (v - w)) & (target // levels == v)
-            mixing += jnp.where(hit, coupling[v, w], 0.0)
+            mixing += jnp.where(hit, rates[3 + v : 4 + v, w : w + 1], 0.0)
     mixer[...] = jnp.concatenate([jnp.concatenate(halves(mixing), axis=1)] * 2, axis=0)
 
     def tendency(field, i, deep, start, size):
@@ -140,18 +142,17 @@
     lax.fori_loop(0, members, member, 0)
 
 
-def forecast(coupling, rates, top, bottom, north, south, west, east, corner_n, corner_s, dests):
+def forecast(rates, top, bottom, north, south, west, east, corner_n, corner_s, dests):
     members, _, cols, entries = top.shape
     cells = 2 * HALO * cols // dests
     return pl.pallas_call(
         forecast_kernel,
-        in_specs=[pl.BlockSpec(memory_space=pltpu.SMEM)] + [pl.BlockSpec()] * 9,
         out_shape=jax.ShapeDtypeStruct((dests, members * cells, entries), jnp.float32),
         scratch_shapes=[pltpu.VMEM((4 * HALO, cols + 2 * EDGE, entries), jnp.float32)] * 2
         + [pltpu.VMEM((2 * entries, 2 * entries), jnp.bfloat16)],
         compiler_params=GRANT,
         name="forecast",
-    )(coupling, rates, top, bottom, north, south, west, east, corner_n, corner_s)
+    )(rates, top, bottom, north, south, west, east, corner_n, corner_s)
 
 
 def weigh_kernel(index, value, weight, total, pulled):
@@ -192,11 +193,13 @@
     return both + dot(al, bh)
 
 
-def analyse_kernel(block, total, pulled, out):
+def analyse_kernel(block, total, pulled, out, spaced, results, sems):
     cells = total.shape[0]
     members = block.shape[0] // cells
     entries = block.shape[1]
     pair = 2 * members
+    for n in range(members):
+        spaced[n * IN_STEP : n * IN_STEP + cells, :] = block[n * cells : (n + 1) * cells, :]
     row_id = lax.broadcasted_iota(jnp.int32, (pair, pair), 0)
     col_id = lax.broadcasted_iota(jnp.int32, (pair, pair), 1)
     eye = (row_id == col_id).astype(jnp.float32)
@@ -206,7 +209,7 @@
     spread = lambda row: jnp.broadcast_to(row, (members, entries))
 
     def first(cell):
-        x = [block[pl.ds(cell + u, members, stride=cells), :] for u in range(2)]
+        x = [spaced[pl.ds(cell + u, members, stride=IN_STEP), :] for u in range(2)]
         mean = [jnp.sum(v, axis=0, keepdims=True) * (1.0 / members) for v in x]
         weight = [total[pl.ds(cell + u, 1), :] for u in range(2)]
         pull = [pulled[pl.ds(cell + u, 1), :] - mean[u] * weight[u] for u in range(2)]
@@ -242,18 +245,23 @@
         rest = (1.0 - jnp.sum(weights, axis=0, keepdims=True)) * (1.0 / members)
         return product(halves(x_turned), halves(weights + rest * same))
 
-    def step(g, carry):
-        cell = [g * (2 * GROUP) + 2 * u for u in range(GROUP)]
+    copies = []
+    span = 2 * GROUP
+    for g in range(cells // span):
+        cell = [g * span + 2 * u for u in range(GROUP)]
         states = [first(c) for c in cell]
         states = [second(s) for s in states]
         states = [third(s) for s in states]
-        results = [fourth(s) for s in states]
-        for c, result in zip(cell, results):
-            out[pl.ds(c, entries, stride=cells), :] = result[:, :members]
-            out[pl.ds(c + 1, entries, stride=cells), :] = result[:, members:]
-        return carry
-
-    lax.fori_loop(0, cells // (2 * GROUP), step, 0)
+        finished = [fourth(s) for s in states]
+        for c, result in zip(cell, finished):
+            results[pl.ds(c, entries, stride=OUT_STEP), :] = result[:, :members]
+            results[pl.ds(c + 1, entries, stride=OUT_STEP), :] = result[:, members:]
+        here = pl.ds(g * span, span)
+        source = results.reshape(entries, OUT_STEP, members).at[:, here, :]
+        copies.append(pltpu.make_async_copy(source, out.at[:, here, :], sems.at[g]))
+        copies[-1].start()
+    for copy in copies:
+        copy.wait()
 
 
 def analyse(block, total, pulled):
@@ -261,7 +269,13 @@
     members = block.shape[0] // cells
     return pl.pallas_call(
         analyse_kernel,
-        out_shape=jax.ShapeDtypeStruct((entries * cells, members), jnp.float32),
+        out_shape=jax.ShapeDtypeStruct((entries, cells, members), jnp.float32),
+        out_specs=pl.BlockSpec(memory_space=pl.ANY),
+        scratch_shapes=[
+            pltpu.VMEM((members * IN_STEP, entries), jnp.float32),
+            pltpu.VMEM((entries * OUT_STEP, members), jnp.float32),
+            pltpu.SemaphoreType.DMA((cells // (2 * GROUP),)),
+        ],
         compiler_params=GRANT,
         name="analyse",
     )(block, total, pulled)
@@ -296,9 +310,14 @@
     corner_n = lax.ppermute(sides[:, HALO:], "row", row_up)
     corner_s = lax.ppermute(sides[:, :HALO], "row", row_down)
 
-    rates = jnp.stack([diffusion, wind_row, wind_col])
+    rates = jnp.concatenate(
+        [
+            jnp.stack([diffusion, wind_row, wind_col]),
+            jnp.pad(coupling, ((0, 0), (0, levels - variables))),
+        ]
+    )
     sent = forecast(
-        coupling, rates, top, bottom, north, south, west, east, corner_n, corner_s, dests
+        rates, top, bottom, north, south, west, east, corner_n, corner_s, dests
     )
     moved = lax.all_to_all(sent, "mem", split_axis=0, concat_axis=0, tiled=True)
     cells = rows * cols // dests

time: 83.4 us -> 78.9 us (0.946)
  Pallas kernels: 13.9 us -> 10.1 us
    pallas_call x2, Pallas kernels: 12.6 us -> 8.76 us  [the longest x1 4.43 us: forecast(): pl.pallas_call(forecast_kernel, out_shape=jax.ShapeDtypeStruct((dests, me...]
    unnamed x10 -> x8, local copies, waits for them, and re-layouts: 1.92 us -> 1.24 us
where the time goes in v1:
time: 78.9 us; the launch traced here: 78.5 us
  waiting for transfers between devices  36.7 us (47%)
  starting transfers between devices  29.6 us (38%)
  Pallas kernels  10.1 us (13%)
  local copies, waits for them, and re-layouts  1.24 us (2%)
    all_to_all x1, waiting for transfers between devices, body(): moved = lax.all_to_all(sent, 'mem', split_axis=0, concat_axis=0, tiled=True)  27.1 us
    all_to_all x1, starting transfers between devices, body(): moved = lax.all_to_all(sent, 'mem', split_axis=0, concat_axis=0, tiled=True)  12 us
    ppermute x1, waiting for transfers between devices, body(): east = lax.ppermute(own_w, 'col', col_down)  7.01 us
    ppermute x1, starting transfers between devices, body(): west = lax.ppermute(own_e, 'col', col_up)  5.81 us
    pallas_call x1, Pallas kernels, forecast(): pl.pallas_call(forecast_kernel, out_shape=jax.ShapeDtypeStruct((dests, me...  4.43 us
    pallas_call x1, Pallas kernels, analyse(): pl.pallas_call(analyse_kernel, out_shape=jax.ShapeDtypeStruct((entries, c...  4.32 us
    ppermute x1, starting transfers between devices, body(): corner_n = lax.ppermute(sides[:, HALO:], 'row', row_up)  3.99 us
    ppermute x1, starting transfers between devices, body(): north = lax.ppermute(bottom, 'row', row_up)  3.97 us
  transfers between devices with their start and end apart: 7, of which 3 were waited for; matrix products, arithmetic and copies ran while one was open for 1% of the time, Pallas kernels for 1%

profile of v1, /device:TPU:1, one launch (start us, length us, event | category | flops | bytes accessed | tf_op | source)
XLA Modules:
  0.0 78.5 jit_solution(9288409204856372164)
XLA Ops:
  0.0 0.0 copy-start
  0.0 1.2 %copy-done = f32[2,4,32,8,128]{4,3,2,1,0:T(8,128)S(1)} copy-done((f32[2,4,32,8,128]{4,3,2,1,0:T(8,128)S(1)}, f32[2,4,32,8,128]{4,3,2,1,0:T(8,128)}, u32[]{:S(2)}) %copy-start) | copy-done | bytes 1048600
  1.2 0.3 turn.1
  1.6 4.0 %collective-permute-start = (f32[2,4,128,128]{3,2,1,0:T(8,128)S(1)}, f32[2,4,128,128]{3,2,1,0:T(8,128)S(1)}, u32[]{:S(2)}, u32[]{:S(2)}) collective-permute-start(f32[2,4,128,128]{3,2,1,0:T(8,128)S(1)} %get-tuple-element.12.bottom), channel_id=1, source_target_pairs={{0,4},{4,8},{8,12},{1,5},{5,9},{9,13},{2,6},{6,10},{10,14},{3,7},{... | collective-permute-start | bytes 1572872 | tf_op jit(solution)/shard_map/ppermute | solution.py:307
  5.5 1.3 %collective-permute-start.1 = (f32[2,4,128,128]{3,2,1,0:T(8,128)S(1)}, f32[2,4,128,128]{3,2,1,0:T(8,128)S(1)}, u32[]{:S(2)}, u32[]{:S(2)}) collective-permute-start(f32[2,4,128,128]{3,2,1,0:T(8,128)S(1)} %get-tuple-element.11.top), channel_id=1, source_target_pairs={{4,0},{8,4},{12,8},{5,1},{9,5},{13,9},{6,2},{10,6},{14,10},{7,3},{... | collective-permute-start | bytes 1572872 | tf_op jit(solution)/shard_map/ppermute | solution.py:308
  6.8 5.8 %collective-permute-start.2 = (f32[2,8,4,128]{3,2,1,0:T(4,128)S(1)}, f32[2,8,4,128]{3,2,1,0:T(4,128)S(1)}, u32[]{:S(2)}, u32[]{:S(2)}) collective-permute-start(f32[2,8,4,128]{3,2,1,0:T(4,128)S(1)} %get-tuple-element.13), channel_id=1, source_target_pairs={{0,1},{1,2},{2,3},{4,5},{5,6},{6,7},{8,9},{9,10},{10,11},{12,13},{... | collective-permute-start | bytes 98312 | tf_op jit(solution)/shard_map/ppermute | solution.py:305
  12.6 1.3 %collective-permute-start.3 = (f32[2,8,4,128]{3,2,1,0:T(4,128)S(1)}, f32[2,8,4,128]{3,2,1,0:T(4,128)S(1)}, u32[]{:S(2)}, u32[]{:S(2)}) collective-permute-start(f32[2,8,4,128]{3,2,1,0:T(4,128)S(1)} %get-tuple-element.14), channel_id=1, source_target_pairs={{1,0},{2,1},{3,2},{5,4},{6,5},{7,6},{9,8},{10,9},{11,10},{13,12},{... | collective-permute-start | bytes 98312 | tf_op jit(solution)/shard_map/ppermute | solution.py:306
  13.9 0.0 collective-permute-done.2.west
  14.0 7.0 %collective-permute-done.3.east = f32[2,8,4,128]{3,2,1,0:T(4,128)S(1)} collective-permute-done((f32[2,8,4,128]{3,2,1,0:T(4,128)S(1)}, f32[2,8,4,128]{3,2,1,0:T(4,128)S(1)}, u32[]{:S(2)}, u32[]{:S(2)}) %collective-permute-start.3) | collective-permute-done | bytes 32800 | tf_op jit(solution)/shard_map/ppermute | solution.py:306
  21.0 4.0 %collective-permute-start.4 = (f32[2,4,8,128]{3,2,1,0:T(8,128)S(1)}, f32[2,4,8,128]{3,2,1,0:T(8,128)S(1)}, u32[]{:S(2)}, u32[]{:S(2)}) collective-permute-start(f32[2,4,8,128]{3,2,1,0:T(8,128)S(1)} %get-tuple-element.18), channel_id=1, source_target_pairs={{0,4},{4,8},{8,12},{1,5},{5,9},{9,13},{2,6},{6,10},{10,14},{3,7},{... | collective-permute-start | bytes 98312 | tf_op jit(solution)/shard_map/ppermute | solution.py:310
  25.0 1.3 %collective-permute-start.5 = (f32[2,4,8,128]{3,2,1,0:T(8,128)S(1)}, f32[2,4,8,128]{3,2,1,0:T(8,128)S(1)}, u32[]{:S(2)}, u32[]{:S(2)}) collective-permute-start(f32[2,4,8,128]{3,2,1,0:T(8,128)S(1)} %get-tuple-element.17), channel_id=1, source_target_pairs={{4,0},{8,4},{12,8},{5,1},{9,5},{13,9},{6,2},{10,6},{14,10},{7,3},{... | collective-permute-start | bytes 98312 | tf_op jit(solution)/shard_map/ppermute | solution.py:311
  26.3 0.7 select_maximum_fusion.rates
  27.0 0.0 copy-start.1
  27.0 0.0 copy-start.2
  27.0 0.0 copy-start.3
  27.0 0.0 collective-permute-done.4.corner_n
  27.0 2.6 %collective-permute-done.5.corner_s = f32[2,4,8,128]{3,2,1,0:T(8,128)S(1)} collective-permute-done((f32[2,4,8,128]{3,2,1,0:T(8,128)S(1)}, f32[2,4,8,128]{3,2,1,0:T(8,128)S(1)}, u32[]{:S(2)}, u32[]{:S(2)}) %collective-permute-start.5) | collective-permute-done | bytes 32800 | tf_op jit(solution)/shard_map/ppermute | solution.py:311
  29.6 0.0 collective-permute-done.north
  29.6 0.0 collective-permute-done.1.south
  29.6 4.4 %forecast.1 = f32[32,64,128]{2,1,0:T(8,128)} custom-call(f32[7,32]{1,0:T(8,128)S(1)} %select_maximum_fusion.rates, f32[2,4,128,128]{3,2,1,0:T(8,128)S(1)} %get-tuple-element.11.top, f32[2,4,128,128]{3,2,1,0:T(8,128)S(1)} %get-tuple-element.12.bottom, f32[2,4,128,128]{3,2,1,0:T(8,128)S(1)} %collective-permute-done.north, ...), custom_call_target="tpu_custom_call" | custom-call | tf_op jit(solution)/shard_map/forecast/pallas_call | solution.py:148
  34.1 12.0 %all-to-all-start = ((f32[32,64,128]{2,1,0:T(8,128)}), f32[32,64,128]{2,1,0:T(8,128)S(1)}, u32[]{:S(2)}, u32[]{:S(2)}) async-start(f32[32,64,128]{2,1,0:T(8,128)} %forecast.1), calls=%async_computation | async-start | bytes 2097152 | tf_op jit(solution)/shard_map/all_to_all | solution.py:322
  46.1 0.0 copy-done.1
  46.1 0.0 copy-done.2
  46.1 0.0 copy-done.3
  46.1 1.0 %weigh.1 = (f32[32,128]{1,0:T(8,128)S(1)}, f32[32,128]{1,0:T(8,128)S(1)}) custom-call(s32[32,64]{1,0:T(8,128)S(1)} %bitcast.19, f32[32,64]{1,0:T(8,128)S(1)} %bitcast.20, f32[32,64]{1,0:T(8,128)S(1)} %bitcast.21), custom_call_target="tpu_custom_call" | custom-call | tf_op jit(solution)/shard_map/weigh/pallas_call | solution.py:177
  47.1 27.1 %all-to-all-done = f32[32,64,128]{2,1,0:T(8,128)S(1)} async-done(((f32[32,64,128]{2,1,0:T(8,128)}), f32[32,64,128]{2,1,0:T(8,128)S(1)}, u32[]{:S(2)}, u32[]{:S(2)}) %all-to-all-start) | async-done | bytes 1048608 | tf_op jit(solution)/shard_map/all_to_all | solution.py:322
  74.1 4.3 %analyse.1 = f32[128,32,64]{2,1,0:T(8,128)} custom-call(f32[2048,128]{1,0:T(8,128)S(1)} %bitcast.17, f32[32,128]{1,0:T(8,128)S(1)} %get-tuple-element.15.total, f32[32,128]{1,0:T(8,128)S(1)} %get-tuple-element.16.pulled), custom_call_target="tpu_custom_call" | custom-call | tf_op jit(solution)/shard_map/analyse/pallas_call | solution.py:270
  (1 shorter events, 0.0 us)
Async XLA Ops:
  0.0 1.2 %copy-start = (f32[2,4,32,8,128]{4,3,2,1,0:T(8,128)S(1)}, f32[2,4,32,8,128]{4,3,2,1,0:T(8,128)}, u32[]{:S(2)}) copy-start(f32[2,4,32,8,128]{4,3,2,1,0:T(8,128)} %param.8) | copy-start | bytes 3145732
  1.6 28.1 %collective-permute-start = (f32[2,4,128,128]{3,2,1,0:T(8,128)S(1)}, f32[2,4,128,128]{3,2,1,0:T(8,128)S(1)}, u32[]{:S(2)}, u32[]{:S(2)}) collective-permute-start(f32[2,4,128,128]{3,2,1,0:T(8,128)S(1)} %get-tuple-element.12.bottom), channel_id=1, source_target_pairs={{0,4},{4,8},{8,12},{1,5},{5,9},{9,13},{2,6},{6,10},{10,14},{3,7},{... | collective-permute-start | bytes 1572872 | tf_op jit(solution)/shard_map/ppermute | solution.py:307
  5.5 24.1 %collective-permute-start.1 = (f32[2,4,128,128]{3,2,1,0:T(8,128)S(1)}, f32[2,4,128,128]{3,2,1,0:T(8,128)S(1)}, u32[]{:S(2)}, u32[]{:S(2)}) collective-permute-start(f32[2,4,128,128]{3,2,1,0:T(8,128)S(1)} %get-tuple-element.11.top), channel_id=1, source_target_pairs={{4,0},{8,4},{12,8},{5,1},{9,5},{13,9},{6,2},{10,6},{14,10},{7,3},{... | collective-permute-start | bytes 1572872 | tf_op jit(solution)/shard_map/ppermute | solution.py:308
  6.8 7.1 %collective-permute-start.2 = (f32[2,8,4,128]{3,2,1,0:T(4,128)S(1)}, f32[2,8,4,128]{3,2,1,0:T(4,128)S(1)}, u32[]{:S(2)}, u32[]{:S(2)}) collective-permute-start(f32[2,8,4,128]{3,2,1,0:T(4,128)S(1)} %get-tuple-element.13), channel_id=1, source_target_pairs={{0,1},{1,2},{2,3},{4,5},{5,6},{6,7},{8,9},{9,10},{10,11},{12,13},{... | collective-permute-start | bytes 98312 | tf_op jit(solution)/shard_map/ppermute | solution.py:305
  12.6 8.3 %collective-permute-start.3 = (f32[2,8,4,128]{3,2,1,0:T(4,128)S(1)}, f32[2,8,4,128]{3,2,1,0:T(4,128)S(1)}, u32[]{:S(2)}, u32[]{:S(2)}) collective-permute-start(f32[2,8,4,128]{3,2,1,0:T(4,128)S(1)} %get-tuple-element.14), channel_id=1, source_target_pairs={{1,0},{2,1},{3,2},{5,4},{6,5},{7,6},{9,8},{10,9},{11,10},{13,12},{... | collective-permute-start | bytes 98312 | tf_op jit(solution)/shard_map/ppermute | solution.py:306
  21.0 6.0 %collective-permute-start.4 = (f32[2,4,8,128]{3,2,1,0:T(8,128)S(1)}, f32[2,4,8,128]{3,2,1,0:T(8,128)S(1)}, u32[]{:S(2)}, u32[]{:S(2)}) collective-permute-start(f32[2,4,8,128]{3,2,1,0:T(8,128)S(1)} %get-tuple-element.18), channel_id=1, source_target_pairs={{0,4},{4,8},{8,12},{1,5},{5,9},{9,13},{2,6},{6,10},{10,14},{3,7},{... | collective-permute-start | bytes 98312 | tf_op jit(solution)/shard_map/ppermute | solution.py:310
  25.0 4.7 %collective-permute-start.5 = (f32[2,4,8,128]{3,2,1,0:T(8,128)S(1)}, f32[2,4,8,128]{3,2,1,0:T(8,128)S(1)}, u32[]{:S(2)}, u32[]{:S(2)}) collective-permute-start(f32[2,4,8,128]{3,2,1,0:T(8,128)S(1)} %get-tuple-element.17), channel_id=1, source_target_pairs={{4,0},{8,4},{12,8},{5,1},{9,5},{13,9},{6,2},{10,6},{14,10},{7,3},{... | collective-permute-start | bytes 98312 | tf_op jit(solution)/shard_map/ppermute | solution.py:311
  27.0 19.1 %copy-start.1 = (s32[64,8,4]{0,2,1:T(4,128)S(1)}, s32[64,8,4]{0,2,1:T(4,128)}, u32[]{:S(2)}) copy-start(s32[64,8,4]{0,2,1:T(4,128)} %param.13) | copy-start | bytes 24580
  27.0 19.1 %copy-start.2 = (f32[64,8,4]{0,2,1:T(4,128)S(1)}, f32[64,8,4]{0,2,1:T(4,128)}, u32[]{:S(2)}) copy-start(f32[64,8,4]{0,2,1:T(4,128)} %param.14) | copy-start | bytes 24580
  27.0 19.1 %copy-start.3 = (f32[64,8,4]{0,2,1:T(4,128)S(1)}, f32[64,8,4]{0,2,1:T(4,128)}, u32[]{:S(2)}) copy-start(f32[64,8,4]{0,2,1:T(4,128)} %param.15) | copy-start | bytes 24580
  34.1 40.1 %all-to-all-start = ((f32[32,64,128]{2,1,0:T(8,128)}), f32[32,64,128]{2,1,0:T(8,128)S(1)}, u32[]{:S(2)}, u32[]{:S(2)}) async-start(f32[32,64,128]{2,1,0:T(8,128)} %forecast.1), calls=%async_computation | async-start | bytes 2097152 | tf_op jit(solution)/shard_map/all_to_all | solution.py:322

commit v2 on v1

--- a/solution.py
+++ b/solution.py
@@ -1,9 +1,12 @@
+import functools
+
 import jax
 import jax.numpy as jnp
 from jax import lax
 from jax.experimental import pallas as pl
 from jax.experimental.pallas import tpu as pltpu
 from jax.sharding import PartitionSpec as P
+
 
 HALO = 4
 EDGE = 16
@@ -15,14 +18,13 @@
 NEWTON = (2.25, -2.4375, 1.6875, -0.5625, 0.0625)
 
 
-def turn_kernel(block, top, bottom, west, east):
+def turn_kernel(block, west, east, *halves_out):
     members, entries, rows, cols = block.shape
     flat = block.reshape(members, entries * rows, cols)
     for m in range(members):
         for i in range(rows):
             plane = flat[m, pl.ds(i, entries, stride=rows), :].T
-            half = top if i < HALO else bottom
-            half[m, i % HALO] = plane
+            halves_out[2 * m + i // HALO][i % HALO] = plane
             west[m, i] = plane[:HALO]
             east[m, i] = plane[cols - HALO :]
 
@@ -30,22 +32,21 @@
 def turn(block):
     members, variables, levels, rows, cols = block.shape
     entries = variables * levels
-    half = jax.ShapeDtypeStruct((members, HALO, cols, entries), jnp.float32)
+    half = jax.ShapeDtypeStruct((HALO, cols, entries), jnp.float32)
     side = jax.ShapeDtypeStruct((members, rows, HALO, entries), jnp.float32)
     return pl.pallas_call(
         turn_kernel,
-        out_shape=[half, half, side, side],
+        out_shape=[side, side] + [half] * (2 * members),
         compiler_params=GRANT,
         name="turn",
     )(block.reshape(members, entries, rows, cols))
 
 
 def forecast_kernel(
-    rates, top, bottom, north, south, west, east, corner_n, corner_s, out, state, slope, mixer
+    m, rates, top, bottom, north, south, west, east, corner_n, corner_s, out, state, slope, mixer
 ):
-    members, _, cols, entries = top.shape
-    dests, listed, _ = out.shape
-    cells = listed // members
+    _, cols, entries = top.shape
+    dests = out.shape[0]
     levels = rates.shape[1]
     variables = entries // levels
     share = cols // dests
@@ -99,7 +100,7 @@
     def rates_of(low, high, deep):
         def step(b, carry):
             i = low + deep * b
-            here, total = tendency(state, i, deep, first, wide)
+            _, total = tendency(state, i, deep, first, wide)
             slope[pl.ds(i, deep), pl.ds(first, wide), :] = masked(total, i)
             return carry
 
@@ -115,44 +116,38 @@
 
         lax.fori_loop(0, (high - low) // deep, step, 0)
 
-    def member(m, carry):
-        for i in range(HALO):
-            state[i, EDGE:last] = north[m, i]
-            state[HALO + i, EDGE:last] = top[m, i]
-            state[2 * HALO + i, EDGE:last] = bottom[m, i]
-            state[3 * HALO + i, EDGE:last] = south[m, i]
-            state[i, EDGE - HALO : EDGE] = corner_n[m, i, :HALO]
-            state[i, last : last + HALO] = corner_n[m, i, HALO:]
-            state[3 * HALO + i, EDGE - HALO : EDGE] = corner_s[m, i, :HALO]
-            state[3 * HALO + i, last : last + HALO] = corner_s[m, i, HALO:]
-        for i in range(rows):
-            state[HALO + i, EDGE - HALO : EDGE] = west[m, i]
-            state[HALO + i, last : last + HALO] = east[m, i]
-        rates_of(1, 15, DEPTH[0])
-        update(2, 14, DEPTH[1])
-        rates_of(3, 13, DEPTH[2])
-        for i in range(0, rows, DEPTH[3]):
-            here, total = tendency(slope, HALO + i, DEPTH[3], EDGE, cols)
-            new = state[HALO + i : HALO + i + DEPTH[3], EDGE:last] + here + 0.5 * total
-            for r in range(DEPTH[3]):
-                for d in range(dests):
-                    out[d, pl.ds(m * cells + (i + r) * share, share), :] = new[r, d * share : (d + 1) * share]
-        return carry
-
-    lax.fori_loop(0, members, member, 0)
-
-
-def forecast(rates, top, bottom, north, south, west, east, corner_n, corner_s, dests):
-    members, _, cols, entries = top.shape
+    for i in range(HALO):
+        for at, rows_here in enumerate((north, top, bottom, south)):
+            state[HALO * at + i, EDGE:last] = rows_here[i]
+        state[i, EDGE - HALO : EDGE] = corner_n[m, i, :HALO]
+        state[i, last : last + HALO] = corner_n[m, i, HALO:]
+        state[3 * HALO + i, EDGE - HALO : EDGE] = corner_s[m, i, :HALO]
+        state[3 * HALO + i, last : last + HALO] = corner_s[m, i, HALO:]
+    for i in range(rows):
+        state[HALO + i, EDGE - HALO : EDGE] = west[m, i]
+        state[HALO + i, last : last + HALO] = east[m, i]
+    rates_of(1, 15, DEPTH[0])
+    update(2, 14, DEPTH[1])
+    rates_of(3, 13, DEPTH[2])
+    for i in range(0, rows, DEPTH[3]):
+        here, total = tendency(slope, HALO + i, DEPTH[3], EDGE, cols)
+        new = state[HALO + i : HALO + i + DEPTH[3], EDGE:last] + here + 0.5 * total
+        for r in range(DEPTH[3]):
+            for d in range(dests):
+                out[d, pl.ds((i + r) * share, share), :] = new[r, d * share : (d + 1) * share]
+
+
+def forecast(m, dests, *operands):
+    _, cols, entries = operands[1].shape
     cells = 2 * HALO * cols // dests
     return pl.pallas_call(
-        forecast_kernel,
-        out_shape=jax.ShapeDtypeStruct((dests, members * cells, entries), jnp.float32),
+        functools.partial(forecast_kernel, m),
+        out_shape=jax.ShapeDtypeStruct((dests, cells, entries), jnp.float32),
         scratch_shapes=[pltpu.VMEM((4 * HALO, cols + 2 * EDGE, entries), jnp.float32)] * 2
         + [pltpu.VMEM((2 * entries, 2 * entries), jnp.bfloat16)],
         compiler_params=GRANT,
         name="forecast",
-    )(rates, top, bottom, north, south, west, east, corner_n, corner_s)
+    )(*operands)
 
 
 def weigh_kernel(index, value, weight, total, pulled):
@@ -193,20 +188,20 @@
     return both + dot(al, bh)
 
 
-def analyse_kernel(block, total, pulled, out, spaced, results, sems):
+def analyse_kernel(blocks, total, pulled, out, spaced, results, sems):
     cells = total.shape[0]
-    members = block.shape[0] // cells
-    entries = block.shape[1]
+    parts = len(blocks)
+    members = parts * blocks[0].shape[0]
+    entries = total.shape[1]
     pair = 2 * members
     for n in range(members):
-        spaced[n * IN_STEP : n * IN_STEP + cells, :] = block[n * cells : (n + 1) * cells, :]
+        spaced[n * IN_STEP : n * IN_STEP + cells, :] = blocks[n % parts][n // parts]
     row_id = lax.broadcasted_iota(jnp.int32, (pair, pair), 0)
     col_id = lax.broadcasted_iota(jnp.int32, (pair, pair), 1)
     eye = (row_id == col_id).astype(jnp.float32)
     same = ((row_id < members) == (col_id < members)).astype(jnp.float32)
     left = lax.broadcasted_iota(jnp.int32, (1, pair), 1) < members
     n0, n1, n2, n3, n4 = NEWTON
-    spread = lambda row: jnp.broadcast_to(row, (members, entries))
 
     def first(cell):
         x = [spaced[pl.ds(cell + u, members, stride=IN_STEP), :] for u in range(2)]
@@ -264,9 +259,9 @@
         copy.wait()
 
 
-def analyse(block, total, pulled):
+def analyse(blocks, total, pulled):
     cells, entries = total.shape
-    members = block.shape[0] // cells
+    members = len(blocks) * blocks[0].shape[0]
     return pl.pallas_call(
         analyse_kernel,
         out_shape=jax.ShapeDtypeStruct((entries, cells, members), jnp.float32),
@@ -278,7 +273,7 @@
         ],
         compiler_params=GRANT,
         name="analyse",
-    )(block, total, pulled)
+    )(blocks, total, pulled)
 
 
 def neighbours(axis):
@@ -299,29 +294,34 @@
     members_here, variables, levels, rows, cols = background_sample.shape
     entries = variables * levels
     dests = lax.axis_size("mem")
-    top, bottom, own_w, own_e = turn(background_sample)
+    own_w, own_e, *own = turn(background_sample)
+    tops, bottoms = (own[0::2], own[1::2])
     col_up, col_down = neighbours("col")
     row_up, row_down = neighbours("row")
     west = lax.ppermute(own_e, "col", col_up)
     east = lax.ppermute(own_w, "col", col_down)
-    north = lax.ppermute(bottom, "row", row_up)
-    south = lax.ppermute(top, "row", row_down)
+    norths = [lax.ppermute(bottoms[0], "row", row_up)]
+    souths = [lax.ppermute(tops[0], "row", row_down)]
     sides = jnp.concatenate([west, east], axis=2)
     corner_n = lax.ppermute(sides[:, HALO:], "row", row_up)
     corner_s = lax.ppermute(sides[:, :HALO], "row", row_down)
-
+    later = (tops[1:], bottoms[1:])
+    later, west, east = lax.optimization_barrier((later, west, east))
+    norths += [lax.ppermute(x, "row", row_up) for x in later[1]]
+    souths += [lax.ppermute(x, "row", row_down) for x in later[0]]
     rates = jnp.concatenate(
         [
             jnp.stack([diffusion, wind_row, wind_col]),
             jnp.pad(coupling, ((0, 0), (0, levels - variables))),
         ]
     )
-    sent = forecast(
-        rates, top, bottom, north, south, west, east, corner_n, corner_s, dests
-    )
-    moved = lax.all_to_all(sent, "mem", split_axis=0, concat_axis=0, tiled=True)
+    moved = []
+    for m in range(members_here):
+        sent = forecast(
+            m, dests, rates, tops[m], bottoms[m], norths[m], souths[m], west, east, corner_n, corner_s
+        )
+        moved.append(lax.all_to_all(sent, "mem", split_axis=0, concat_axis=0, tiled=True))
     cells = rows * cols // dests
-    members = dests * members_here
 
     def listed(x):
         return jnp.transpose(x, (1, 2, 0)).reshape(cells, x.shape[0])
@@ -329,13 +329,14 @@
     total, pulled = weigh(
         listed(observed_entry_index), listed(obs_value), listed(obs_weight), entries
     )
-    result = analyse(moved.reshape(members * cells, entries), total, pulled)
-    result = result.reshape(variables, levels, rows, cols // dests, members)
+    result = analyse(moved, total, pulled)
+    result = result.reshape(variables, levels, rows, cols // dests, dests * members_here)
     return jnp.transpose(result, (4, 0, 1, 2, 3))
 
 
 def solution(mesh):
     obs = P(None, "row", ("col", "mem"))
+
     return jax.shard_map(
         body,
         mesh=mesh,

time: 78.9 us -> 88.9 us (1.13)
  starting transfers between devices: 29.6 us -> 44 us
  waiting for transfers between devices: 36.7 us -> 31.6 us
    all_to_all x1 -> x2, waiting for transfers between devices: 27.1 us -> 16.4 us  [body(): lax.all_to_all(sent, 'mem', split_axis=0, concat_axis=0, tiled=True)]
    all_to_all x1 -> x2, starting transfers between devices: 12 us -> 20.2 us  [body(): lax.all_to_all(sent, 'mem', split_axis=0, concat_axis=0, tiled=True)]
    ppermute x2 -> x4, waiting for transfers between devices: 0.01 us -> 7.95 us  [the longest x1 4.1 us: body(): norths += [lax.ppermute(x, 'row', row_up) for x in later[1]]]
    ppermute x2 -> x4, starting transfers between devices: 5.26 us -> 11.1 us  [the longest x1 4.58 us: body(): norths = [lax.ppermute(bottoms[0], 'row', row_up)]]
    ppermute x1, waiting for transfers between devices: 2.6 us -> 0.01 us  [body(): corner_s = lax.ppermute(sides[:, :HALO], 'row', row_down)]
    pallas_call x2 -> x3, Pallas kernels: 4.76 us -> 5.32 us  [the longest x2 4.99 us: forecast(): pl.pallas_call(functools.partial(forecast_kernel, m), out_shape=jax.Shape...]
  transfers between devices with their start and end apart: 7 -> 10, of which waited for: 3 -> 6; matrix products, arithmetic and copies ran while one was open for 1% -> 1% of each run, Pallas kernels for 1% -> 4%
where the time goes in v2:
time: 88.9 us; the launch traced here: 88.3 us
  starting transfers between devices  44 us (49%)
  waiting for transfers between devices  31.6 us (36%)
  Pallas kernels  10.6 us (12%)
  local copies, waits for them, and re-layouts  1.24 us (1%)
    all_to_all x2, starting transfers between devices, body(): lax.all_to_all(sent, 'mem', split_axis=0, concat_axis=0, tiled=True)  20.2 us
    all_to_all x2, waiting for transfers between devices, body(): lax.all_to_all(sent, 'mem', split_axis=0, concat_axis=0, tiled=True)  16.4 us
    ppermute x1, waiting for transfers between devices, body(): east = lax.ppermute(own_w, 'col', col_down)  7.01 us
    ppermute x1, starting transfers between devices, body(): west = lax.ppermute(own_e, 'col', col_up)  6.05 us
    pallas_call x2, Pallas kernels, forecast(): pl.pallas_call(functools.partial(forecast_kernel, m), out_shape=jax.Shape...  4.99 us
    ppermute x1, starting transfers between devices, body(): norths = [lax.ppermute(bottoms[0], 'row', row_up)]  4.58 us
    pallas_call x1, Pallas kernels, analyse(): pl.pallas_call(analyse_kernel, out_shape=jax.ShapeDtypeStruct((entries, c...  4.33 us
    ppermute x1, waiting for transfers between devices, body(): norths += [lax.ppermute(x, 'row', row_up) for x in later[1]]  4.1 us
  transfers between devices with their start and end apart: 10, of which 6 were waited for; matrix products, arithmetic and copies ran while one was open for 1% of the time, Pallas kernels for 4%

profile of v2, /device:TPU:1, one launch (start us, length us, event | category | flops | bytes accessed | tf_op | source)
XLA Modules:
  0.0 88.3 jit_solution(7499926398658436068)
XLA Ops:
  0.0 0.0 copy-start
  0.0 1.2 %copy-done = f32[2,4,32,8,128]{4,3,2,1,0:T(8,128)S(1)} copy-done((f32[2,4,32,8,128]{4,3,2,1,0:T(8,128)S(1)}, f32[2,4,32,8,128]{4,3,2,1,0:T(8,128)}, u32[]{:S(2)}) %copy-start) | copy-done | bytes 1048600
  1.2 0.3 turn.1
  1.6 1.3 %collective-permute-start.1 = (f32[4,128,128]{2,1,0:T(8,128)S(1)}, f32[4,128,128]{2,1,0:T(8,128)S(1)}, u32[]{:S(2)}, u32[]{:S(2)}) collective-permute-start(f32[4,128,128]{2,1,0:T(8,128)S(1)} %get-tuple-element.17.top), channel_id=1, source_target_pairs={{4,0},{8,4},{12,8},{5,1},{9,5},{13,9},{6,2},{10,6},{14,10},{7,3},{... | collective-permute-start | bytes 786440 | tf_op jit(solution)/shard_map/ppermute | solution.py:304
  2.9 4.6 %collective-permute-start = (f32[4,128,128]{2,1,0:T(8,128)S(1)}, f32[4,128,128]{2,1,0:T(8,128)S(1)}, u32[]{:S(2)}, u32[]{:S(2)}) collective-permute-start(f32[4,128,128]{2,1,0:T(8,128)S(1)} %get-tuple-element.18.bottom), channel_id=1, source_target_pairs={{0,4},{4,8},{8,12},{1,5},{5,9},{9,13},{2,6},{6,10},{10,14},{3,7},{... | collective-permute-start | bytes 786440 | tf_op jit(solution)/shard_map/ppermute | solution.py:303
  7.4 6.0 %collective-permute-start.2 = (f32[2,8,4,128]{3,2,1,0:T(4,128)S(1)}, f32[2,8,4,128]{3,2,1,0:T(4,128)S(1)}, u32[]{:S(2)}, u32[]{:S(2)}) collective-permute-start(f32[2,8,4,128]{3,2,1,0:T(4,128)S(1)} %get-tuple-element.21), channel_id=1, source_target_pairs={{0,1},{1,2},{2,3},{4,5},{5,6},{6,7},{8,9},{9,10},{10,11},{12,13},{... | collective-permute-start | bytes 98312 | tf_op jit(solution)/shard_map/ppermute | solution.py:301
  13.5 1.3 %collective-permute-start.3 = (f32[2,8,4,128]{3,2,1,0:T(4,128)S(1)}, f32[2,8,4,128]{3,2,1,0:T(4,128)S(1)}, u32[]{:S(2)}, u32[]{:S(2)}) collective-permute-start(f32[2,8,4,128]{3,2,1,0:T(4,128)S(1)} %get-tuple-element.22), channel_id=1, source_target_pairs={{1,0},{2,1},{3,2},{5,4},{6,5},{7,6},{9,8},{10,9},{11,10},{13,12},{... | collective-permute-start | bytes 98312 | tf_op jit(solution)/shard_map/ppermute | solution.py:302
  14.8 0.0 collective-permute-done.2.west
  14.8 7.0 %collective-permute-done.3.east = f32[2,8,4,128]{3,2,1,0:T(4,128)S(1)} collective-permute-done((f32[2,8,4,128]{3,2,1,0:T(4,128)S(1)}, f32[2,8,4,128]{3,2,1,0:T(4,128)S(1)}, u32[]{:S(2)}, u32[]{:S(2)}) %collective-permute-start.3) | collective-permute-done | bytes 32800 | tf_op jit(solution)/shard_map/ppermute | solution.py:302
  21.8 1.3 %collective-permute-start.5 = (f32[2,4,8,128]{3,2,1,0:T(8,128)S(1)}, f32[2,4,8,128]{3,2,1,0:T(8,128)S(1)}, u32[]{:S(2)}, u32[]{:S(2)}) collective-permute-start(f32[2,4,8,128]{3,2,1,0:T(8,128)S(1)} %get-tuple-element.29), channel_id=1, source_target_pairs={{4,0},{8,4},{12,8},{5,1},{9,5},{13,9},{6,2},{10,6},{14,10},{7,3},{... | collective-permute-start | bytes 98312 | tf_op jit(solution)/shard_map/ppermute | solution.py:307
  23.1 4.0 %collective-permute-start.4 = (f32[2,4,8,128]{3,2,1,0:T(8,128)S(1)}, f32[2,4,8,128]{3,2,1,0:T(8,128)S(1)}, u32[]{:S(2)}, u32[]{:S(2)}) collective-permute-start(f32[2,4,8,128]{3,2,1,0:T(8,128)S(1)} %get-tuple-element.30), channel_id=1, source_target_pairs={{0,4},{4,8},{8,12},{1,5},{5,9},{9,13},{2,6},{6,10},{10,14},{3,7},{... | collective-permute-start | bytes 98312 | tf_op jit(solution)/shard_map/ppermute | solution.py:306
  27.1 0.7 select_maximum_fusion.rates
  27.9 0.0 collective-permute-done.5.corner_s
  27.9 0.3 collective-permute-done.4.corner_n
  28.1 0.0 collective-permute-done.1.south
  28.1 0.0 collective-permute-done.north
  28.1 2.5 %forecast.2 = f32[32,32,128]{2,1,0:T(8,128)} custom-call(f32[7,32]{1,0:T(8,128)S(1)} %select_maximum_fusion.rates, f32[4,128,128]{2,1,0:T(8,128)S(1)} %get-tuple-element.17.top, f32[4,128,128]{2,1,0:T(8,128)S(1)} %get-tuple-element.18.bottom, f32[4,128,128]{2,1,0:T(8,128)S(1)} %collective-permute-done.north, ...), custom_call_target="tpu_custom_call" | custom-call | tf_op jit(solution)/shard_map/forecast/pallas_call | solution.py:143
  30.6 0.0 copy-start.1
  30.7 0.0 copy-start.2
  30.7 0.0 copy-start.3
  30.7 11.8 %all-to-all-start = ((f32[32,32,128]{2,1,0:T(8,128)}), f32[32,32,128]{2,1,0:T(8,128)S(1)}, u32[]{:S(2)}, u32[]{:S(2)}) async-start(f32[32,32,128]{2,1,0:T(8,128)} %forecast.2), calls=%async_computation | async-start | bytes 1048576 | tf_op jit(solution)/shard_map/all_to_all | solution.py:323
  42.5 4.0 %collective-permute-start.6 = (f32[4,128,128]{2,1,0:T(8,128)S(1)}, f32[4,128,128]{2,1,0:T(8,128)S(1)}, u32[]{:S(2)}, u32[]{:S(2)}) collective-permute-start(f32[4,128,128]{2,1,0:T(8,128)S(1)} %get-tuple-element.25.bottom), channel_id=1, source_target_pairs={{0,4},{4,8},{8,12},{1,5},{5,9},{9,13},{2,6},{6,10},{10,14},{3,7},{... | collective-permute-start | bytes 786440 | tf_op jit(solution)/shard_map/ppermute | solution.py:310
  46.4 1.3 %collective-permute-start.7 = (f32[4,128,128]{2,1,0:T(8,128)S(1)}, f32[4,128,128]{2,1,0:T(8,128)S(1)}, u32[]{:S(2)}, u32[]{:S(2)}) collective-permute-start(f32[4,128,128]{2,1,0:T(8,128)S(1)} %get-tuple-element.26.top), channel_id=1, source_target_pairs={{4,0},{8,4},{12,8},{5,1},{9,5},{13,9},{6,2},{10,6},{14,10},{7,3},{... | collective-permute-start | bytes 786440 | tf_op jit(solution)/shard_map/ppermute | solution.py:311
  47.7 4.1 %collective-permute-done.6.north = f32[4,128,128]{2,1,0:T(8,128)S(1)} collective-permute-done((f32[4,128,128]{2,1,0:T(8,128)S(1)}, f32[4,128,128]{2,1,0:T(8,128)S(1)}, u32[]{:S(2)}, u32[]{:S(2)}) %collective-permute-start.6) | collective-permute-done | bytes 262176 | tf_op jit(solution)/shard_map/ppermute | solution.py:310
  51.8 3.8 %collective-permute-done.7.south = f32[4,128,128]{2,1,0:T(8,128)S(1)} collective-permute-done((f32[4,128,128]{2,1,0:T(8,128)S(1)}, f32[4,128,128]{2,1,0:T(8,128)S(1)}, u32[]{:S(2)}, u32[]{:S(2)}) %collective-permute-start.7) | collective-permute-done | bytes 262176 | tf_op jit(solution)/shard_map/ppermute | solution.py:311
  55.7 2.5 %forecast.3 = f32[32,32,128]{2,1,0:T(8,128)} custom-call(f32[7,32]{1,0:T(8,128)S(1)} %select_maximum_fusion.rates, f32[4,128,128]{2,1,0:T(8,128)S(1)} %get-tuple-element.26.top, f32[4,128,128]{2,1,0:T(8,128)S(1)} %get-tuple-element.25.bottom, f32[4,128,128]{2,1,0:T(8,128)S(1)} %collective-permute-done.6.north, ...), custom_call_target="tpu_custom_call" | custom-call | tf_op jit(solution)/shard_map/forecast/pallas_call | solution.py:143
  58.2 0.9 all-to-all-done.blocks_0_
  59.0 8.4 %all-to-all-start.1 = ((f32[32,32,128]{2,1,0:T(8,128)}), f32[32,32,128]{2,1,0:T(8,128)S(1)}, u32[]{:S(2)}, u32[]{:S(2)}) async-start(f32[32,32,128]{2,1,0:T(8,128)} %forecast.3), calls=%async_computation.1 | async-start | bytes 1048576 | tf_op jit(solution)/shard_map/all_to_all | solution.py:323
  67.4 0.0 copy-done.1
  67.4 0.0 copy-done.2
  67.5 0.0 copy-done.3
  67.5 1.0 %weigh.1 = (f32[32,128]{1,0:T(8,128)S(1)}, f32[32,128]{1,0:T(8,128)S(1)}) custom-call(s32[32,64]{1,0:T(8,128)S(1)} %bitcast.17, f32[32,64]{1,0:T(8,128)S(1)} %bitcast.18, f32[32,64]{1,0:T(8,128)S(1)} %bitcast.19), custom_call_target="tpu_custom_call" | custom-call | tf_op jit(solution)/shard_map/weigh/pallas_call | solution.py:172
  68.5 15.5 %all-to-all-done.1.blocks_1_ = f32[32,32,128]{2,1,0:T(8,128)S(1)} async-done(((f32[32,32,128]{2,1,0:T(8,128)}), f32[32,32,128]{2,1,0:T(8,128)S(1)}, u32[]{:S(2)}, u32[]{:S(2)}) %all-to-all-start.1) | async-done | bytes 524320 | tf_op jit(solution)/shard_map/all_to_all | solution.py:323
  84.0 4.3 %analyse.1 = f32[128,32,64]{2,1,0:T(8,128)} custom-call(f32[32,32,128]{2,1,0:T(8,128)S(1)} %all-to-all-done.blocks_0_, f32[32,32,128]{2,1,0:T(8,128)S(1)} %all-to-all-done.1.blocks_1_, f32[32,128]{1,0:T(8,128)S(1)} %get-tuple-element.27.total, f32[32,128]{1,0:T(8,128)S(1)} %get-tuple-element.28.pulled), custom_call_target="tpu_custom_call" | custom-call | tf_op jit(solution)/shard_map/analyse/pallas_call | solution.py:265
  (1 shorter events, 0.0 us)
Async XLA Ops:
  0.0 1.2 %copy-start = (f32[2,4,32,8,128]{4,3,2,1,0:T(8,128)S(1)}, f32[2,4,32,8,128]{4,3,2,1,0:T(8,128)}, u32[]{:S(2)}) copy-start(f32[2,4,32,8,128]{4,3,2,1,0:T(8,128)} %param.8) | copy-start | bytes 3145732
  1.6 26.6 %collective-permute-start.1 = (f32[4,128,128]{2,1,0:T(8,128)S(1)}, f32[4,128,128]{2,1,0:T(8,128)S(1)}, u32[]{:S(2)}, u32[]{:S(2)}) collective-permute-start(f32[4,128,128]{2,1,0:T(8,128)S(1)} %get-tuple-element.17.top), channel_id=1, source_target_pairs={{4,0},{8,4},{12,8},{5,1},{9,5},{13,9},{6,2},{10,6},{14,10},{7,3},{... | collective-permute-start | bytes 786440 | tf_op jit(solution)/shard_map/ppermute | solution.py:304
  2.9 25.3 %collective-permute-start = (f32[4,128,128]{2,1,0:T(8,128)S(1)}, f32[4,128,128]{2,1,0:T(8,128)S(1)}, u32[]{:S(2)}, u32[]{:S(2)}) collective-permute-start(f32[4,128,128]{2,1,0:T(8,128)S(1)} %get-tuple-element.18.bottom), channel_id=1, source_target_pairs={{0,4},{4,8},{8,12},{1,5},{5,9},{9,13},{2,6},{6,10},{10,14},{3,7},{... | collective-permute-start | bytes 786440 | tf_op jit(solution)/shard_map/ppermute | solution.py:303
  7.4 7.4 %collective-permute-start.2 = (f32[2,8,4,128]{3,2,1,0:T(4,128)S(1)}, f32[2,8,4,128]{3,2,1,0:T(4,128)S(1)}, u32[]{:S(2)}, u32[]{:S(2)}) collective-permute-start(f32[2,8,4,128]{3,2,1,0:T(4,128)S(1)} %get-tuple-element.21), channel_id=1, source_target_pairs={{0,1},{1,2},{2,3},{4,5},{5,6},{6,7},{8,9},{9,10},{10,11},{12,13},{... | collective-permute-start | bytes 98312 | tf_op jit(solution)/shard_map/ppermute | solution.py:301
  13.5 8.3 %collective-permute-start.3 = (f32[2,8,4,128]{3,2,1,0:T(4,128)S(1)}, f32[2,8,4,128]{3,2,1,0:T(4,128)S(1)}, u32[]{:S(2)}, u32[]{:S(2)}) collective-permute-start(f32[2,8,4,128]{3,2,1,0:T(4,128)S(1)} %get-tuple-element.22), channel_id=1, source_target_pairs={{1,0},{2,1},{3,2},{5,4},{6,5},{7,6},{9,8},{10,9},{11,10},{13,12},{... | collective-permute-start | bytes 98312 | tf_op jit(solution)/shard_map/ppermute | solution.py:302
  21.8 6.0 %collective-permute-start.5 = (f32[2,4,8,128]{3,2,1,0:T(8,128)S(1)}, f32[2,4,8,128]{3,2,1,0:T(8,128)S(1)}, u32[]{:S(2)}, u32[]{:S(2)}) collective-permute-start(f32[2,4,8,128]{3,2,1,0:T(8,128)S(1)} %get-tuple-element.29), channel_id=1, source_target_pairs={{4,0},{8,4},{12,8},{5,1},{9,5},{13,9},{6,2},{10,6},{14,10},{7,3},{... | collective-permute-start | bytes 98312 | tf_op jit(solution)/shard_map/ppermute | solution.py:307
  23.1 5.0 %collective-permute-start.4 = (f32[2,4,8,128]{3,2,1,0:T(8,128)S(1)}, f32[2,4,8,128]{3,2,1,0:T(8,128)S(1)}, u32[]{:S(2)}, u32[]{:S(2)}) collective-permute-start(f32[2,4,8,128]{3,2,1,0:T(8,128)S(1)} %get-tuple-element.30), channel_id=1, source_target_pairs={{0,4},{4,8},{8,12},{1,5},{5,9},{9,13},{2,6},{6,10},{10,14},{3,7},{... | collective-permute-start | bytes 98312 | tf_op jit(solution)/shard_map/ppermute | solution.py:306
  30.6 36.8 %copy-start.1 = (s32[64,8,4]{0,2,1:T(4,128)S(1)}, s32[64,8,4]{0,2,1:T(4,128)}, u32[]{:S(2)}) copy-start(s32[64,8,4]{0,2,1:T(4,128)} %param.13) | copy-start | bytes 24580
  30.7 36.8 %copy-start.2 = (f32[64,8,4]{0,2,1:T(4,128)S(1)}, f32[64,8,4]{0,2,1:T(4,128)}, u32[]{:S(2)}) copy-start(f32[64,8,4]{0,2,1:T(4,128)} %param.14) | copy-start | bytes 24580
  30.7 36.8 %copy-start.3 = (f32[64,8,4]{0,2,1:T(4,128)S(1)}, f32[64,8,4]{0,2,1:T(4,128)}, u32[]{:S(2)}) copy-start(f32[64,8,4]{0,2,1:T(4,128)} %param.15) | copy-start | bytes 24580
  30.7 28.4 %all-to-all-start = ((f32[32,32,128]{2,1,0:T(8,128)}), f32[32,32,128]{2,1,0:T(8,128)S(1)}, u32[]{:S(2)}, u32[]{:S(2)}) async-start(f32[32,32,128]{2,1,0:T(8,128)} %forecast.2), calls=%async_computation | async-start | bytes 1048576 | tf_op jit(solution)/shard_map/all_to_all | solution.py:323
  42.5 9.4 %collective-permute-start.6 = (f32[4,128,128]{2,1,0:T(8,128)S(1)}, f32[4,128,128]{2,1,0:T(8,128)S(1)}, u32[]{:S(2)}, u32[]{:S(2)}) collective-permute-start(f32[4,128,128]{2,1,0:T(8,128)S(1)} %get-tuple-element.25.bottom), channel_id=1, source_target_pairs={{0,4},{4,8},{8,12},{1,5},{5,9},{9,13},{2,6},{6,10},{10,14},{3,7},{... | collective-permute-start | bytes 786440 | tf_op jit(solution)/shard_map/ppermute | solution.py:310
  46.4 9.2 %collective-permute-start.7 = (f32[4,128,128]{2,1,0:T(8,128)S(1)}, f32[4,128,128]{2,1,0:T(8,128)S(1)}, u32[]{:S(2)}, u32[]{:S(2)}) collective-permute-start(f32[4,128,128]{2,1,0:T(8,128)S(1)} %get-tuple-element.26.top), channel_id=1, source_target_pairs={{4,0},{8,4},{12,8},{5,1},{9,5},{13,9},{6,2},{10,6},{14,10},{7,3},{... | collective-permute-start | bytes 786440 | tf_op jit(solution)/shard_map/ppermute | solution.py:311
  59.0 25.0 %all-to-all-start.1 = ((f32[32,32,128]{2,1,0:T(8,128)}), f32[32,32,128]{2,1,0:T(8,128)S(1)}, u32[]{:S(2)}, u32[]{:S(2)}) async-start(f32[32,32,128]{2,1,0:T(8,128)} %forecast.3), calls=%async_computation.1 | async-start | bytes 1048576 | tf_op jit(solution)/shard_map/all_to_all | solution.py:323
